TPU v7x, 32 devices: a whole 2x2x4 slice. The times are simulated.
32 devices in a mesh: dp: 4 (over z), expert: 8 (over y, x, core).
Axes of the slice: x: 2, y: 2, z: 4, core: 2. Of those that a mesh axis runs over, the one named last changes fastest.
Arguments:
- tokens: bfloat16 [256, 192, 1024], P(None, ('dp', 'expert')), may hold values from -200 to 200
- grad_out: bfloat16 [256, 192, 1024], P(None, ('dp', 'expert')), may hold values from -6 to 6
- slot_out: bfloat16 [512, 192, 1024], P('expert', 'dp'), may hold values from -6 to 6
- slot_params: bfloat16 [512, 1024], P('expert'), may hold values from -2 to 2
Outputs:
- grad_tokens: bfloat16 [256, 192, 1024], P(None, ('dp', 'expert'))
- grad_slot_out: bfloat16 [512, 192, 1024], P('expert', 'dp')
- grad_params: float32 [512, 1024], P('expert', 'dp')
All inputs are finite; a program needn't handle non-finite values.
Results may differ from a plain program's by a relative error of at most 0.018.
Values may be sent and summed in bfloat16 or wider, within the bound.
A program may use at most 128 MiB of HBM per device.

v0:
```python
import jax
import jax.numpy as jnp
from jax import lax
from jax.sharding import PartitionSpec as P


def fetch_outputs(slot_out, owners):
    own_slots, img_all, width = slot_out.shape
    shaped = slot_out.reshape(own_slots, owners, img_all // owners, width)
    arrived = lax.all_to_all(shaped, "expert", split_axis=1, concat_axis=0, tiled=True)
    return arrived.reshape(own_slots * owners, img_all // owners, width)


def return_grads(grad_slot, owners):
    all_slots, img_rows, width = grad_slot.shape
    shaped = grad_slot.reshape(owners, all_slots // owners, img_rows, width)
    arrived = lax.all_to_all(shaped, "expert", split_axis=0, concat_axis=2, tiled=True)
    return arrived.reshape(all_slots // owners, owners * img_rows, width)


def logit_grads(grad_comb, combine):
    rowdot = jnp.sum(combine * grad_comb, axis=-1, keepdims=True)
    return (combine * (grad_comb - rowdot)).astype(jnp.bfloat16)


def per_device(tokens, grad_out, slot_out, slot_params):
    owners = lax.axis_size("expert")
    all_params = lax.all_gather(slot_params, "expert", axis=0, tiled=True)
    logits = jnp.einsum("tbd,sd->tbs", tokens, all_params, preferred_element_type=jnp.float32)
    combine = jax.nn.softmax(logits, axis=-1)
    combine_low = combine.astype(jnp.bfloat16)
    slot_rows = fetch_outputs(slot_out, owners)
    grad_slot = jnp.einsum(
        "tbs,tbd->sbd", combine_low, grad_out, preferred_element_type=jnp.float32
    ).astype(jnp.bfloat16)
    grad_slot_out = return_grads(grad_slot, owners)
    grad_comb = jnp.einsum("tbd,sbd->tbs", grad_out, slot_rows, preferred_element_type=jnp.float32)
    grad_logits = logit_grads(grad_comb, combine)
    grad_tok = jnp.einsum(
        "tbs,sd->tbd", grad_logits, all_params, preferred_element_type=jnp.float32
    ).astype(jnp.bfloat16)
    param_part = jnp.einsum("tbs,tbd->sd", grad_logits, tokens, preferred_element_type=jnp.float32)
    owned = lax.psum_scatter(
        param_part.astype(jnp.bfloat16), "expert", scatter_dimension=0, tiled=True
    )
    grad_params = lax.psum_scatter(owned, "dp", scatter_dimension=1, tiled=True).astype(jnp.float32)
    return (grad_tok, grad_slot_out, grad_params)


def solution(mesh):
    return jax.shard_map(
        per_device,
        mesh=mesh,
        in_specs=(
            P(None, ("dp", "expert"), None),
            P(None, ("dp", "expert"), None),
            P("expert", "dp", None),
            P("expert", None),
        ),
        out_specs=(P(None, ("dp", "expert"), None), P("expert", "dp", None), P("expert", "dp")),
        check_vma=False,
    )
```

profile of v0, /device:TPU:0, one launch (start us, length us, event | category | flops | bytes accessed | tf_op | source)
XLA Modules:
  0.0 202.6 jit_solution(12654161094282766128)
XLA Ops:
  7.2 0.0 copy-start
  7.2 9.1 %copy.12 = bf16[64,48,1024]{2,0,1:T(8,128)(2,1)} copy(bf16[64,48,1024]{2,1,0:T(8,128)(2,1)} %param.6) | data formatting | bytes 12582912 | tf_op args[2]
  16.3 5.2 %all-to-all-start = ((bf16[64,8,6,1024]{3,0,2,1:T(8,128)(2,1)}), bf16[64,8,6,1024]{3,0,2,1:T(8,128)(2,1)}, u32[]{:S(2)}, u32[]{:S(2)}) async-start(bf16[64,8,6,1024]{3,0,2,1:T(8,128)(2,1)} %bitcast.38), calls=%async_computation | async-start | bytes 12582912 | tf_op jit(solution)/shard_map/all_to_all | solution.py:10
  21.5 0.0 all-gather.2.cloned.1.call-start
  21.6 0.7 all-gather.2.cloned.1.call-update
  22.3 45.9 %all-gather.2.cloned.1.call-done = bf16[512,1024]{1,0:T(8,128)(2,1)} async-done(((bf16[64,1024]{1,0:T(8,128)(2,1)}), bf16[512,1024]{1,0:T(8,128)(2,1)}) %all-gather.2.cloned.1.call-update) | async-done | bytes 1048592 | tf_op jit(solution)/shard_map/all_gather | solution.py:28
  68.2 4.1 %fusion.6 = f32[256,6,512]{2,0,1:T(8,128)S(1)} fusion(bf16[256,6,1024]{2,0,1:T(8,128)(2,1)} %param.4, bf16[512,1024]{1,0:T(8,128)(2,1)} %all-gather.2.cloned.1.call-done), kind=kOutput, calls=%fused_computation.13 | convolution fusion | flops 1610612736 | bytes 7340032 | tf_op jit(solution)/shard_map/tbd,sd->tbs/dot_general | solution.py:29
  72.3 0.0 copy-start.2
  72.3 2.5 %fusion.8 = (f32[256,6]{0,1:T(8,128)S(1)}, f32[256,6,512]{2,0,1:T(8,128)}) fusion(f32[256,6,512]{2,0,1:T(8,128)S(1)} %fusion.6), kind=kOutput, calls=%fused_computation.15 | output fusion | flops 1573375 | bytes 6297600 | tf_op jit(solution)/shard_map/sub | solution.py:30
  74.8 0.1 copy-done.2
  74.9 0.0 copy-done
  74.9 11.4 %convolution_convert_fusion = bf16[6,512,1024]{2,1,0:T(8,128)(2,1)} fusion(bf16[256,6,1024]{2,0,1:T(8,128)(2,1)S(1)} %copy-done, f32[256,6]{0,1:T(8,128)S(1)} %get-tuple-element.6, f32[256,6,512]{2,0,1:T(8,128)} %copy-done.2), kind=kOutput, calls=%fused_computation.1 | convolution fusion | flops 1616119808 | bytes 12589056 | tf_op jit(solution)/shard_map/tbs,tbd->sbd/dot_general | solution.py:33
  86.3 6.7 %copy.16 = bf16[8,64,6,1024]{3,1,2,0:T(8,128)(2,1)} copy(bf16[8,64,6,1024]{3,1,0,2:T(8,128)(2,1)} %bitcast.40) | data formatting | bytes 12582912 | tf_op jit(solution)/shard_map/reshape | solution.py:16
  93.0 4.6 %all-to-all-done = bf16[64,8,6,1024]{3,0,2,1:T(8,128)(2,1)} async-done(((bf16[64,8,6,1024]{3,0,2,1:T(8,128)(2,1)}), bf16[64,8,6,1024]{3,0,2,1:T(8,128)(2,1)}, u32[]{:S(2)}, u32[]{:S(2)}) %all-to-all-start) | async-done | bytes 6291488 | tf_op jit(solution)/shard_map/all_to_all | solution.py:10
  97.6 4.8 %all-to-all-start.1 = ((bf16[8,64,6,1024]{3,1,2,0:T(8,128)(2,1)}), bf16[8,64,6,1024]{3,1,2,0:T(8,128)(2,1)}, u32[]{:S(2)}, u32[]{:S(2)}) async-start(bf16[8,64,6,1024]{3,1,2,0:T(8,128)(2,1)} %copy.16), calls=%async_computation.1 | async-start | bytes 12582912 | tf_op jit(solution)/shard_map/all_to_all | solution.py:17
  102.4 0.2 reduce-scatter.3.cloned.1.call-start
  102.6 0.0 copy-start.1
  102.7 3.7 %copy.13 = bf16[8,64,1,6,1024]{4,1,0,3,2:T(8,128)(2,1)S(1)} copy(bf16[8,64,1,6,1024]{4,1,3,0,2:T(8,128)(2,1)} %bitcast.3) | data formatting | bytes 12582912 | tf_op jit(solution)/shard_map/all_to_all | solution.py:10
  106.3 0.0 copy-done.1
  106.4 2.0 fusion.1
  108.3 0.0 copy-start.4
  108.3 0.6 fusion.3
  109.0 0.0 copy-start.3
  109.0 1.1 copy-done.3
  110.1 0.7 copy-done.4
  110.8 2.8 %bitcast_convert_fusion = bf16[512,1024]{1,0:T(8,128)(2,1)} fusion(bf16[256,6,512]{2,0,1:T(8,128)(2,1)S(1)} %fusion.3, bf16[256,6,1024]{2,0,1:T(8,128)(2,1)S(1)} %copy-done.4), kind=kOutput, calls=%fused_computation.9 | convolution fusion | flops 1611137024 | bytes 5767168 | tf_op jit(solution)/shard_map/tbs,tbd->sd/dot_general | solution.py:42
  113.6 0.0 reduce-scatter.3.cloned.1.call-update
  113.6 0.0 reduce-scatter.5.cloned.1.call-start
  113.7 60.1 %reduce-scatter.3.cloned.1.call-done = bf16[64,1024]{1,0:T(8,128)(2,1)} async-done(((bf16[512,1024]{1,0:T(8,128)(2,1)}), bf16[64,1024]{1,0:T(8,128)(2,1)}) %reduce-scatter.3.cloned.1.call-update) | async-done | bytes 131088 | tf_op jit(solution)/shard_map/reduce_scatter | solution.py:43
  173.8 0.0 reduce-scatter.5.cloned.1.call-update
  173.8 5.2 %convolution_convert_fusion.1 = bf16[256,6,1024]{2,0,1:T(8,128)(2,1)} fusion(bf16[256,6,512]{2,0,1:T(8,128)(2,1)} %copy-done.3, bf16[512,1024]{1,0:T(8,128)(2,1)} %all-gather.2.cloned.1.call-done), kind=kOutput, calls=%fused_computation.8 | convolution fusion | flops 1612185600 | bytes 5767168 | tf_op jit(solution)/shard_map/tbs,sd->tbd/dot_general | solution.py:39
  179.0 0.0 all-to-all-done.1
  179.0 9.0 %copy.18 = bf16[64,48,1024]{2,1,0:T(8,128)(2,1)} copy(bf16[64,48,1024]{2,0,1:T(8,128)(2,1)} %bitcast.10) | data formatting | bytes 12582912
  188.0 6.6 %reduce-scatter.5.cloned.1.call-done = bf16[64,256]{1,0:T(8,128)(2,1)} async-done(((bf16[64,1024]{1,0:T(8,128)(2,1)}), bf16[64,256]{1,0:T(8,128)(2,1)}) %reduce-scatter.5.cloned.1.call-update) | async-done | bytes 32784 | tf_op jit(solution)/shard_map/reduce_scatter | solution.py:46
  194.6 1.4 convert_element_type.27
Async XLA Ops:
  7.2 67.7 %copy-start = (bf16[256,6,1024]{2,0,1:T(8,128)(2,1)S(1)}, bf16[256,6,1024]{2,0,1:T(8,128)(2,1)}, u32[]{:S(2)}) copy-start(bf16[256,6,1024]{2,0,1:T(8,128)(2,1)} %param.5) | copy-start | bytes 9437188
  16.3 81.3 %all-to-all-start = ((bf16[64,8,6,1024]{3,0,2,1:T(8,128)(2,1)}), bf16[64,8,6,1024]{3,0,2,1:T(8,128)(2,1)}, u32[]{:S(2)}, u32[]{:S(2)}) async-start(bf16[64,8,6,1024]{3,0,2,1:T(8,128)(2,1)} %bitcast.38), calls=%async_computation | async-start | bytes 12582912 | tf_op jit(solution)/shard_map/all_to_all | solution.py:10
  21.5 46.6 %all-gather.2.cloned.1.call-start = ((), (), s32[]{:S(2)}) async-start(), calls=%async_computation.4 | async-start | bytes 1179648 | tf_op jit(solution)/shard_map/all_gather | solution.py:28
  72.3 2.7 %copy-start.2 = (f32[256,6,512]{2,0,1:T(8,128)}, f32[256,6,512]{2,0,1:T(8,128)S(1)}, u32[]{:S(2)}) copy-start(f32[256,6,512]{2,0,1:T(8,128)S(1)} %fusion.6) | copy-start | bytes 9437188
  97.6 81.4 %all-to-all-start.1 = ((bf16[8,64,6,1024]{3,1,2,0:T(8,128)(2,1)}), bf16[8,64,6,1024]{3,1,2,0:T(8,128)(2,1)}, u32[]{:S(2)}, u32[]{:S(2)}) async-start(bf16[8,64,6,1024]{3,1,2,0:T(8,128)(2,1)} %copy.16), calls=%async_computation.1 | async-start | bytes 12582912 | tf_op jit(solution)/shard_map/all_to_all | solution.py:17
  102.4 71.4 %reduce-scatter.3.cloned.1.call-start = ((), (), s32[]{:S(2)}) async-start(), calls=%async_computation.5 | async-start | bytes 1179648 | tf_op jit(solution)/shard_map/reduce_scatter | solution.py:43
  102.6 3.7 %copy-start.1 = (f32[256,6,512]{2,0,1:T(8,128)S(1)}, f32[256,6,512]{2,0,1:T(8,128)}, u32[]{:S(2)}) copy-start(f32[256,6,512]{2,0,1:T(8,128)} %get-tuple-element.7) | copy-start | bytes 9437188
  108.3 2.5 %copy-start.4 = (bf16[256,6,1024]{2,0,1:T(8,128)(2,1)S(1)}, bf16[256,6,1024]{2,0,1:T(8,128)(2,1)}, u32[]{:S(2)}) copy-start(bf16[256,6,1024]{2,0,1:T(8,128)(2,1)} %param.4) | copy-start | bytes 9437188
  109.0 1.1 copy-start.3
  113.6 81.0 %reduce-scatter.5.cloned.1.call-start = ((), (), s32[]{:S(2)}) async-start(), calls=%async_computation.6 | async-start | bytes 163840 | tf_op jit(solution)/shard_map/reduce_scatter | solution.py:46
Sparse Core Ops, SparseCore 0:
  24.2 43.8 all-gather.1
  113.7 60.0 reduce-scatter.2
  176.0 18.5 reduce-scatter.4
where the time goes:
time: 203 us
  waiting for transfers between devices  118 us (58%)
  local copies, waits for them, and re-layouts  30.5 us (15%)
  matrix products  25.4 us (13%)
  between operations  13.8 us (7%)
  starting transfers between devices  10.3 us (5%)
  other arithmetic  4.54 us (2%)
    reduce_scatter x1, waiting for transfers between devices, per_device(): lax.psum_scatter(param_part.astype(jnp.bfloat16), 'expert', scatter_dimen...  60.1 us
    all_gather x1, waiting for transfers between devices, per_device(): all_params = lax.all_gather(slot_params, 'expert', axis=0, tiled=True)  45.9 us
    unnamed x12, local copies, waits for them, and re-layouts  20.2 us
    dot_general x1, matrix products, per_device(): jnp.einsum('tbs,tbd->sbd', combine_low, grad_out, preferred_element_type=...  11.4 us
    reshape x1, local copies, waits for them, and re-layouts, return_grads(): shaped = grad_slot.reshape(owners, all_slots // owners, img_rows, width)  6.69 us
    reduce_scatter x1, waiting for transfers between devices, per_device(): lax.psum_scatter(owned, 'dp', scatter_dimension=1, tiled=True)  6.62 us
    all_to_all x1, starting transfers between devices, fetch_outputs(): lax.all_to_all(shaped, 'expert', split_axis=1, concat_axis=0, tiled=True)  5.2 us
    dot_general x1, matrix products, per_device(): jnp.einsum('tbs,sd->tbd', grad_logits, all_params, preferred_element_type...  5.17 us
  transfers between devices with their start and end apart: 5, of which 4 were waited for; matrix products, arithmetic and copies ran while one was open for 24% of the time, Pallas kernels for 0%

commit v1 on v0

--- a/solution.py
+++ b/solution.py
@@ -25,7 +25,14 @@
 
 def per_device(tokens, grad_out, slot_out, slot_params):
     owners = lax.axis_size("expert")
-    all_params = lax.all_gather(slot_params, "expert", axis=0, tiled=True)
+    ring = [slot_params]
+    for hop in range(7):
+        ring.append(lax.ppermute(ring[-1], "expert", [(dev, (dev + 1) % 8) for dev in range(8)]))
+    all_params = jnp.roll(
+        jnp.concatenate(ring[::-1], axis=0),
+        (lax.axis_index("expert") + 1) * ring[0].shape[0],
+        axis=0,
+    )
     logits = jnp.einsum("tbd,sd->tbs", tokens, all_params, preferred_element_type=jnp.float32)
     combine = jax.nn.softmax(logits, axis=-1)
     combine_low = combine.astype(jnp.bfloat16)

time: 203 us -> 260 us (1.28)
  waiting for transfers between devices: 118 us -> 172 us
  local copies, waits for them, and re-layouts: 30.5 us -> 38.8 us
  matrix products: 25.4 us -> 19.1 us
    ppermute x0 -> x7, waiting for transfers between devices: none -> 105 us  [per_device(): lax.ppermute(ring[-1], 'expert', [(dev, (dev + 1) % 8) for dev in range(8)])]
    all_gather x1 -> x0, waiting for transfers between devices: 45.9 us -> none  [per_device(): all_params = lax.all_gather(slot_params, 'expert', axis=0, tiled=True)]
    unnamed x12 -> x45, local copies, waits for them, and re-layouts: 20.2 us -> 28.4 us
    all_to_all x1, waiting for transfers between devices: 4.6 us -> 0.01 us  [fetch_outputs(): lax.all_to_all(shaped, 'expert', split_axis=1, concat_axis=0, tiled=True)]
    dot_general x1, matrix products: 11.4 us -> 7.33 us  [per_device(): jnp.einsum('tbs,tbd->sbd', combine_low, grad_out, preferred_element_type=...]
  transfers between devices with their start and end apart: 5 -> 11, of which waited for: 4 -> 9; matrix products, arithmetic and copies ran while one was open for 24% -> 19% of each run, Pallas kernels for 0% -> 0%
where the time goes in v1:
time: 260 us; the launch traced here: 259 us
  waiting for transfers between devices  172 us (66%)
  local copies, waits for them, and re-layouts  38.8 us (15%)
  matrix products  19.1 us (7%)
  between operations  14.3 us (6%)
  starting transfers between devices  10.9 us (4%)
  other arithmetic  4.78 us (2%)
    ppermute x7, waiting for transfers between devices, per_device(): lax.ppermute(ring[-1], 'expert', [(dev, (dev + 1) % 8) for dev in range(8)])  105 us
    reduce_scatter x1, waiting for transfers between devices, per_device(): lax.psum_scatter(param_part.astype(jnp.bfloat16), 'expert', scatter_dimen...  60.2 us
    unnamed x45, local copies, waits for them, and re-layouts  28.4 us
    dot_general x1, matrix products, per_device(): jnp.einsum('tbs,tbd->sbd', combine_low, grad_out, preferred_element_type=...  7.33 us
    reshape x1, local copies, waits for them, and re-layouts, return_grads(): shaped = grad_slot.reshape(owners, all_slots // owners, img_rows, width)  6.68 us
    reduce_scatter x1, waiting for transfers between devices, per_device(): lax.psum_scatter(owned, 'dp', scatter_dimension=1, tiled=True)  6.55 us
    all_to_all x1, starting transfers between devices, fetch_outputs(): lax.all_to_all(shaped, 'expert', split_axis=1, concat_axis=0, tiled=True)  5.33 us
    dot_general x1, matrix products, per_device(): jnp.einsum('tbs,sd->tbd', grad_logits, all_params, preferred_element_type...  5.2 us
  transfers between devices with their start and end apart: 11, of which 9 were waited for; matrix products, arithmetic and copies ran while one was open for 19% of the time, Pallas kernels for 0%

profile of v1, /device:TPU:0, one launch (start us, length us, event | category | flops | bytes accessed | tf_op | source)
XLA Modules:
  0.0 259.4 jit_solution(9543488815251218017)
XLA Ops:
  7.2 0.0 copy-start
  7.2 9.1 %copy.10 = bf16[64,48,1024]{2,0,1:T(8,128)(2,1)} copy(bf16[64,48,1024]{2,1,0:T(8,128)(2,1)} %param.6) | data formatting | bytes 12582912 | tf_op args[2]
  16.3 5.3 %all-to-all-start = ((bf16[64,8,6,1024]{3,0,2,1:T(8,128)(2,1)}), bf16[64,8,6,1024]{3,0,2,1:T(8,128)(2,1)}, u32[]{:S(2)}, u32[]{:S(2)}) async-start(bf16[64,8,6,1024]{3,0,2,1:T(8,128)(2,1)} %bitcast.55), calls=%async_computation | async-start | bytes 12582912 | tf_op jit(solution)/shard_map/all_to_all | solution.py:10
  21.7 0.0 copy-done.4
  21.7 0.5 collective-permute-start
  22.2 72.6 %collective-permute-done = bf16[64,1024]{1,0:T(8,128)(2,1)S(1)} collective-permute-done((bf16[64,1024]{1,0:T(8,128)(2,1)S(1)}, bf16[64,1024]{1,0:T(8,128)(2,1)S(1)}, u32[]{:S(2)}, u32[]{:S(2)}) %collective-permute-start) | collective-permute-done | bytes 131104 | tf_op jit(solution)/shard_map/ppermute | solution.py:30
  94.8 0.0 collective-permute-start.1
  94.8 5.3 %collective-permute-done.1 = bf16[64,1024]{1,0:T(8,128)(2,1)S(1)} collective-permute-done((bf16[64,1024]{1,0:T(8,128)(2,1)S(1)}, bf16[64,1024]{1,0:T(8,128)(2,1)S(1)}, u32[]{:S(2)}, u32[]{:S(2)}) %collective-permute-start.1) | collective-permute-done | bytes 131104 | tf_op jit(solution)/shard_map/ppermute | solution.py:30
  100.1 0.0 collective-permute-start.2
  100.1 5.3 %collective-permute-done.2 = bf16[64,1024]{1,0:T(8,128)(2,1)S(1)} collective-permute-done((bf16[64,1024]{1,0:T(8,128)(2,1)S(1)}, bf16[64,1024]{1,0:T(8,128)(2,1)S(1)}, u32[]{:S(2)}, u32[]{:S(2)}) %collective-permute-start.2) | collective-permute-done | bytes 131104 | tf_op jit(solution)/shard_map/ppermute | solution.py:30
  105.4 0.6 copy-done.5
  106.0 0.0 collective-permute-start.3
  106.0 5.3 %collective-permute-done.3 = bf16[64,1024]{1,0:T(8,128)(2,1)S(1)} collective-permute-done((bf16[64,1024]{1,0:T(8,128)(2,1)S(1)}, bf16[64,1024]{1,0:T(8,128)(2,1)S(1)}, u32[]{:S(2)}, u32[]{:S(2)}) %collective-permute-start.3) | collective-permute-done | bytes 131104 | tf_op jit(solution)/shard_map/ppermute | solution.py:30
  111.3 0.6 copy-done.7
  112.0 0.0 collective-permute-start.4
  112.0 5.3 %collective-permute-done.4 = bf16[64,1024]{1,0:T(8,128)(2,1)S(1)} collective-permute-done((bf16[64,1024]{1,0:T(8,128)(2,1)S(1)}, bf16[64,1024]{1,0:T(8,128)(2,1)S(1)}, u32[]{:S(2)}, u32[]{:S(2)}) %collective-permute-start.4) | collective-permute-done | bytes 131104 | tf_op jit(solution)/shard_map/ppermute | solution.py:30
  117.3 0.7 copy-done.9
  117.9 0.0 collective-permute-start.5
  117.9 5.4 %collective-permute-done.5 = bf16[64,1024]{1,0:T(8,128)(2,1)} collective-permute-done((bf16[64,1024]{1,0:T(8,128)(2,1)S(1)}, bf16[64,1024]{1,0:T(8,128)(2,1)}, u32[]{:S(2)}, u32[]{:S(2)}) %collective-permute-start.5) | collective-permute-done | bytes 131104 | tf_op jit(solution)/shard_map/ppermute | solution.py:30
  123.3 0.0 collective-permute-start.6
  123.3 0.0 copy-start.12
  123.3 5.6 %collective-permute-done.6 = bf16[64,1024]{1,0:T(8,128)(2,1)} collective-permute-done((bf16[64,1024]{1,0:T(8,128)(2,1)}, bf16[64,1024]{1,0:T(8,128)(2,1)}, u32[]{:S(2)}, u32[]{:S(2)}) %collective-permute-start.6) | collective-permute-done | bytes 131104 | tf_op jit(solution)/shard_map/ppermute | solution.py:30
  128.9 0.9 constant_dynamic-update-slice_fusion.15
  129.8 0.9 constant_dynamic-update-slice_fusion.14
  130.8 0.9 constant_dynamic-update-slice_fusion.13
  131.7 0.9 constant_dynamic-update-slice_fusion.12
  132.6 0.9 constant_dynamic-update-slice_fusion.11
  133.6 0.9 constant_dynamic-update-slice_fusion.7
  134.5 0.9 constant_dynamic-update-slice_fusion.6
  135.4 0.0 copy-done.10
  135.4 0.0 copy-done.8
  135.5 0.0 copy-done.6
  135.5 0.0 copy-done.12
  135.6 0.0 copy-start.11
  135.6 1.8 fusion.10
  137.4 0.0 copy-done.11
  137.4 0.0 copy-start.2
  137.4 2.7 %fusion.20 = (f32[256,6]{0,1:T(8,128)S(1)}, f32[256,6,512]{0,2,1:T(8,128)}) fusion(f32[512,256,6]{1,0,2:T(8,128)S(1)} %fusion.10), kind=kOutput, calls=%fused_computation.38 | output fusion | flops 1573375 | bytes 6297600 | tf_op jit(solution)/shard_map/sub | solution.py:37
  140.1 0.0 copy-done.2
  140.1 0.0 copy-done
  140.1 7.3 %convolution_convert_fusion = bf16[6,512,1024]{2,1,0:T(8,128)(2,1)} fusion(bf16[256,6,1024]{2,0,1:T(8,128)(2,1)S(1)} %copy-done, f32[256,6]{0,1:T(8,128)S(1)} %get-tuple-element.6, f32[512,256,6]{1,0,2:T(8,128)} %copy-done.2), kind=kOutput, calls=%fused_computation.1 | convolution fusion | flops 1616119808 | bytes 12589056 | tf_op jit(solution)/shard_map/tbs,tbd->sbd/dot_general | solution.py:40
  147.5 6.7 %copy.13 = bf16[8,64,6,1024]{3,1,2,0:T(8,128)(2,1)} copy(bf16[8,64,6,1024]{3,1,0,2:T(8,128)(2,1)} %bitcast.57) | data formatting | bytes 12582912 | tf_op jit(solution)/shard_map/reshape | solution.py:16
  154.1 0.0 all-to-all-done
  154.1 4.8 %all-to-all-start.1 = ((bf16[8,64,6,1024]{3,1,2,0:T(8,128)(2,1)}), bf16[8,64,6,1024]{3,1,2,0:T(8,128)(2,1)}, u32[]{:S(2)}, u32[]{:S(2)}) async-start(bf16[8,64,6,1024]{3,1,2,0:T(8,128)(2,1)} %copy.13), calls=%async_computation.1 | async-start | bytes 12582912 | tf_op jit(solution)/shard_map/all_to_all | solution.py:17
  159.0 0.2 reduce-scatter.3.cloned.1.call-start
  159.2 0.0 copy-start.1
  159.2 3.7 %copy.11 = bf16[8,64,1,6,1024]{4,1,0,3,2:T(8,128)(2,1)S(1)} copy(bf16[8,64,1,6,1024]{4,1,3,0,2:T(8,128)(2,1)} %bitcast.4) | data formatting | bytes 12582912 | tf_op jit(solution)/shard_map/all_to_all | solution.py:10
  162.9 0.0 copy-done.1
  162.9 1.9 fusion.1
  164.8 0.0 copy-start.13
  164.8 0.7 fusion.3
  165.5 0.0 copy-start.3
  165.6 1.1 copy-done.3
  166.7 0.6 copy-done.13
  167.3 2.8 %bitcast_convert_fusion = bf16[512,1024]{1,0:T(8,128)(2,1)} fusion(bf16[256,6,512]{0,2,1:T(8,128)(2,1)S(1)} %fusion.3, bf16[256,6,1024]{2,0,1:T(8,128)(2,1)S(1)} %copy-done.13), kind=kOutput, calls=%fused_computation.12 | convolution fusion | flops 1611137024 | bytes 5767168 | tf_op jit(solution)/shard_map/tbs,tbd->sd/dot_general | solution.py:49
  170.1 0.0 reduce-scatter.3.cloned.1.call-update
  170.1 0.0 reduce-scatter.5.cloned.1.call-start
  170.1 60.2 %reduce-scatter.3.cloned.1.call-done = bf16[64,1024]{1,0:T(8,128)(2,1)} async-done(((bf16[512,1024]{1,0:T(8,128)(2,1)}), bf16[64,1024]{1,0:T(8,128)(2,1)}) %reduce-scatter.3.cloned.1.call-update) | async-done | bytes 131088 | tf_op jit(solution)/shard_map/reduce_scatter | solution.py:50
  230.4 0.0 reduce-scatter.5.cloned.1.call-update
  230.4 5.2 %convolution_convert_fusion.1 = bf16[256,6,1024]{2,0,1:T(8,128)(2,1)} fusion(bf16[256,6,512]{0,2,1:T(8,128)(2,1)} %copy-done.3, bf16[1024,1024]{1,0:T(8,128)(2,1)} %copy-done.11, s32[]{:T(128)S(6)} %select_n.14), kind=kOutput, calls=%fused_computation.11 | convolution fusion | flops 1612185600 | bytes 5767172 | tf_op jit(solution)/shard_map/tbs,sd->tbd/dot_general | solution.py:46
  235.6 0.0 all-to-all-done.1
  235.6 9.0 %copy.14 = bf16[64,48,1024]{2,1,0:T(8,128)(2,1)} copy(bf16[64,48,1024]{2,0,1:T(8,128)(2,1)} %bitcast.11) | data formatting | bytes 12582912
  244.6 6.5 %reduce-scatter.5.cloned.1.call-done = bf16[64,256]{1,0:T(8,128)(2,1)} async-done(((bf16[64,1024]{1,0:T(8,128)(2,1)}), bf16[64,256]{1,0:T(8,128)(2,1)}) %reduce-scatter.5.cloned.1.call-update) | async-done | bytes 32784 | tf_op jit(solution)/shard_map/reduce_scatter | solution.py:53
  251.1 1.4 convert_element_type.27
  (16 shorter events, 0.1 us)
Async XLA Ops:
  7.2 133.0 %copy-start = (bf16[256,6,1024]{2,0,1:T(8,128)(2,1)S(1)}, bf16[256,6,1024]{2,0,1:T(8,128)(2,1)}, u32[]{:S(2)}) copy-start(bf16[256,6,1024]{2,0,1:T(8,128)(2,1)} %param.5) | copy-start | bytes 9437188
  16.3 5.3 %copy-start.4 = (bf16[64,1024]{1,0:T(8,128)(2,1)S(1)}, bf16[64,1024]{1,0:T(8,128)(2,1)}, u32[]{:S(2)}) copy-start(bf16[64,1024]{1,0:T(8,128)(2,1)} %param.7) | copy-start | bytes 393220
  16.3 137.8 %all-to-all-start = ((bf16[64,8,6,1024]{3,0,2,1:T(8,128)(2,1)}), bf16[64,8,6,1024]{3,0,2,1:T(8,128)(2,1)}, u32[]{:S(2)}, u32[]{:S(2)}) async-start(bf16[64,8,6,1024]{3,0,2,1:T(8,128)(2,1)} %bitcast.55), calls=%async_computation | async-start | bytes 12582912 | tf_op jit(solution)/shard_map/all_to_all | solution.py:10
  21.7 73.1 %collective-permute-start = (bf16[64,1024]{1,0:T(8,128)(2,1)S(1)}, bf16[64,1024]{1,0:T(8,128)(2,1)S(1)}, u32[]{:S(2)}, u32[]{:S(2)}) collective-permute-start(bf16[64,1024]{1,0:T(8,128)(2,1)S(1)} %copy-done.4), channel_id=1, source_target_pairs={{0,1},{1,2},{2,3},{3,4},{4,5},{5,6},{6,7},{7,0},{8,9},{9,10},{10,1... | collective-permute-start | bytes 393224 | tf_op jit(solution)/shard_map/ppermute | solution.py:30
  94.8 5.3 %collective-permute-start.1 = (bf16[64,1024]{1,0:T(8,128)(2,1)S(1)}, bf16[64,1024]{1,0:T(8,128)(2,1)S(1)}, u32[]{:S(2)}, u32[]{:S(2)}) collective-permute-start(bf16[64,1024]{1,0:T(8,128)(2,1)S(1)} %collective-permute-done), channel_id=1, source_target_pairs={{0,1},{1,2},{2,3},{3,4},{4,5},{5,6},{6,7},{7,0},{8,9},{9,10},{10,1... | collective-permute-start | bytes 393224 | tf_op jit(solution)/shard_map/ppermute | solution.py:30
  100.1 5.3 %collective-permute-start.2 = (bf16[64,1024]{1,0:T(8,128)(2,1)S(1)}, bf16[64,1024]{1,0:T(8,128)(2,1)S(1)}, u32[]{:S(2)}, u32[]{:S(2)}) collective-permute-start(bf16[64,1024]{1,0:T(8,128)(2,1)S(1)} %collective-permute-done.1), channel_id=1, source_target_pairs={{0,1},{1,2},{2,3},{3,4},{4,5},{5,6},{6,7},{7,0},{8,9},{9,10},{10,1... | collective-permute-start | bytes 393224 | tf_op jit(solution)/shard_map/ppermute | solution.py:30
  105.4 0.7 copy-start.5
  106.0 5.3 %collective-permute-start.3 = (bf16[64,1024]{1,0:T(8,128)(2,1)S(1)}, bf16[64,1024]{1,0:T(8,128)(2,1)S(1)}, u32[]{:S(2)}, u32[]{:S(2)}) collective-permute-start(bf16[64,1024]{1,0:T(8,128)(2,1)S(1)} %collective-permute-done.2), channel_id=1, source_target_pairs={{0,1},{1,2},{2,3},{3,4},{4,5},{5,6},{6,7},{7,0},{8,9},{9,10},{10,1... | collective-permute-start | bytes 393224 | tf_op jit(solution)/shard_map/ppermute | solution.py:30
  111.3 0.7 copy-start.7
  112.0 5.3 %collective-permute-start.4 = (bf16[64,1024]{1,0:T(8,128)(2,1)S(1)}, bf16[64,1024]{1,0:T(8,128)(2,1)S(1)}, u32[]{:S(2)}, u32[]{:S(2)}) collective-permute-start(bf16[64,1024]{1,0:T(8,128)(2,1)S(1)} %collective-permute-done.3), channel_id=1, source_target_pairs={{0,1},{1,2},{2,3},{3,4},{4,5},{5,6},{6,7},{7,0},{8,9},{9,10},{10,1... | collective-permute-start | bytes 393224 | tf_op jit(solution)/shard_map/ppermute | solution.py:30
  117.3 0.7 copy-start.9
  117.9 5.4 %collective-permute-start.5 = (bf16[64,1024]{1,0:T(8,128)(2,1)S(1)}, bf16[64,1024]{1,0:T(8,128)(2,1)}, u32[]{:S(2)}, u32[]{:S(2)}) collective-permute-start(bf16[64,1024]{1,0:T(8,128)(2,1)S(1)} %collective-permute-done.4), channel_id=1, source_target_pairs={{0,1},{1,2},{2,3},{3,4},{4,5},{5,6},{6,7},{7,0},{8,9},{9,10},{10,1... | collective-permute-start | bytes 393224 | tf_op jit(solution)/shard_map/ppermute | solution.py:30
  123.3 5.6 %collective-permute-start.6 = (bf16[64,1024]{1,0:T(8,128)(2,1)}, bf16[64,1024]{1,0:T(8,128)(2,1)}, u32[]{:S(2)}, u32[]{:S(2)}) collective-permute-start(bf16[64,1024]{1,0:T(8,128)(2,1)} %collective-permute-done.5), channel_id=1, source_target_pairs={{0,1},{1,2},{2,3},{3,4},{4,5},{5,6},{6,7},{7,0},{8,9},{9,10},{10,1... | collective-permute-start | bytes 393224 | tf_op jit(solution)/shard_map/ppermute | solution.py:30
  123.3 12.1 %copy-start.10 = (bf16[64,1024]{1,0:T(8,128)(2,1)S(1)}, bf16[64,1024]{1,0:T(8,128)(2,1)}, u32[]{:S(2)}) copy-start(bf16[64,1024]{1,0:T(8,128)(2,1)} %copy-done.9) | copy-start | bytes 393220
  123.3 12.1 %copy-start.8 = (bf16[64,1024]{1,0:T(8,128)(2,1)S(1)}, bf16[64,1024]{1,0:T(8,128)(2,1)}, u32[]{:S(2)}) copy-start(bf16[64,1024]{1,0:T(8,128)(2,1)} %copy-done.7) | copy-start | bytes 393220
  123.3 12.1 %copy-start.6 = (bf16[64,1024]{1,0:T(8,128)(2,1)S(1)}, bf16[64,1024]{1,0:T(8,128)(2,1)}, u32[]{:S(2)}) copy-start(bf16[64,1024]{1,0:T(8,128)(2,1)} %copy-done.5) | copy-start | bytes 393220
  123.3 12.2 %copy-start.12 = (bf16[256,6,1024]{2,0,1:T(8,128)(2,1)S(1)}, bf16[256,6,1024]{2,0,1:T(8,128)(2,1)}, u32[]{:S(2)}) copy-start(bf16[256,6,1024]{2,0,1:T(8,128)(2,1)} %param.4) | copy-start | bytes 9437188
  135.6 1.9 copy-start.11
  137.4 2.7 %copy-start.2 = (f32[512,256,6]{1,0,2:T(8,128)}, f32[512,256,6]{1,0,2:T(8,128)S(1)}, u32[]{:S(2)}) copy-start(f32[512,256,6]{1,0,2:T(8,128)S(1)} %fusion.10) | copy-start | bytes 9437188
  154.1 81.4 %all-to-all-start.1 = ((bf16[8,64,6,1024]{3,1,2,0:T(8,128)(2,1)}), bf16[8,64,6,1024]{3,1,2,0:T(8,128)(2,1)}, u32[]{:S(2)}, u32[]{:S(2)}) async-start(bf16[8,64,6,1024]{3,1,2,0:T(8,128)(2,1)} %copy.13), calls=%async_computation.1 | async-start | bytes 12582912 | tf_op jit(solution)/shard_map/all_to_all | solution.py:17
  159.0 71.4 %reduce-scatter.3.cloned.1.call-start = ((), (), s32[]{:S(2)}) async-start(), calls=%async_computation.4 | async-start | bytes 1179648 | tf_op jit(solution)/shard_map/reduce_scatter | solution.py:50
  159.2 3.7 %copy-start.1 = (f32[256,6,512]{0,2,1:T(8,128)S(1)}, f32[256,6,512]{0,2,1:T(8,128)}, u32[]{:S(2)}) copy-start(f32[256,6,512]{0,2,1:T(8,128)} %get-tuple-element.7) | copy-start | bytes 9437188
  164.8 2.4 copy-start.13
  165.5 1.1 copy-start.3
  170.1 81.1 %reduce-scatter.5.cloned.1.call-start = ((), (), s32[]{:S(2)}) async-start(), calls=%async_computation.5 | async-start | bytes 163840 | tf_op jit(solution)/shard_map/reduce_scatter | solution.py:53
Sparse Core Ops, SparseCore 0:
  170.2 60.0 reduce-scatter.2
  232.6 18.5 reduce-scatter.4
